TPU v7x, 32 devices: a whole 2x2x4 slice. The times are simulated.
32 devices in a mesh: blk: 8 (over y, x, core), rel: 4 (over z).
Axes of the slice: x: 2, y: 2, z: 4, core: 2. Of those that a mesh axis runs over, the one named last changes fastest.
Arguments:
- features: bfloat16 [4096, 512], P(('blk', 'rel')), may hold values from -6 to 6
- adjacency: int32 [6, 128, 4, 1024], P(None, 'blk', 'rel'), may hold values from -2147483648 to 2147483646, as said below
- tile_mask: int32 [6, 32, 8, 4], P(None, 'blk', None, 'rel'), may hold values from 0 to 1
- bases: bfloat16 [512, 8, 512], P('rel'), may hold values from -0.25 to 0.25
- coefficients: float32 [6, 8], replicated, may hold values from -2 to 2
- self_weight: bfloat16 [512, 512], P('rel'), may hold values from -0.25 to 0.25
Outputs:
- updated: bfloat16 [4096, 512], P(('blk', 'rel'))
Inputs may be any that keep to these rules, and one draw needn't show every extreme that they name: `adjacency`: each word holds 32 edge bits, bit t for destination node 32 * word index + t.
All inputs are finite; a program needn't handle non-finite values.
Results may differ from a plain program's by a relative error of at most 0.0058.
Values may be sent and summed in bfloat16 or wider, within the bound.
A program may use at most 64 MiB of HBM per device.

v0:
```python
import jax
import jax.numpy as jnp
from jax import lax
from jax.sharding import PartitionSpec as P


def expand_edges(packed, tile_flags):
    shifts = jnp.arange(32, dtype=jnp.int32)
    edge_bits = jnp.bitwise_and(
        jnp.right_shift(packed[:, :, None, :], shifts[None, None, :, None]), 1
    )
    edge_bits = edge_bits.reshape(packed.shape[0], packed.shape[1] * 32, packed.shape[2])
    tile_rows = jnp.repeat(tile_flags, 128, axis=1)
    return edge_bits * tile_rows


def shards(features, adjacency, tile_mask, bases, coefficients, self_weight):
    relations = adjacency.shape[0]
    words = adjacency.shape[1]
    blocks = tile_mask.shape[2]
    sub_rows = features.shape[0]
    width = features.shape[1]
    full_bases, self_full = (
        lax.all_gather(bases, "rel", axis=0, tiled=True),
        lax.all_gather(self_weight, "rel", axis=0, tiled=True),
    )
    rel_weight = jnp.einsum(
        "rb,ibj->irj", coefficients, full_bases.astype(jnp.float32), precision=lax.Precision.HIGHEST
    ).astype(jnp.bfloat16)
    weight_all = rel_weight.reshape(width, relations * width)
    packed_all = adjacency.reshape(relations, words, blocks * sub_rows)
    flags_all = jnp.repeat(
        tile_mask.reshape(relations, tile_mask.shape[1], blocks), sub_rows, axis=2
    )
    portion = lax.all_gather(features, "blk", axis=0, tiled=True)
    values = jnp.dot(portion, weight_all, preferred_element_type=jnp.float32).astype(jnp.bfloat16)
    aggregate_values = values.reshape(portion.shape[0], relations, width)
    edges = expand_edges(packed_all, flags_all)
    degree = jnp.sum(edges, axis=(0, 2)).astype(jnp.float32)
    edges = edges.astype(jnp.bfloat16)
    running = jnp.einsum("rns,srd->nd", edges, aggregate_values, preferred_element_type=jnp.float32)
    message, degree = (running, degree)
    message, degree = (
        lax.psum_scatter(message, "rel", scatter_dimension=0, tiled=True),
        lax.psum_scatter(degree, "rel", scatter_dimension=0, tiled=True),
    )
    own = jnp.dot(features, self_full, preferred_element_type=jnp.float32)
    return jax.nn.relu(own + message * lax.rsqrt(1.0 + degree)[:, None]).astype(jnp.bfloat16)


def solution(mesh):
    placed = (
        P(("blk", "rel"), None),
        P(None, "blk", "rel", None),
        P(None, "blk", None, "rel"),
        P("rel", None, None),
        P(),
        P("rel", None),
    )
    return jax.shard_map(
        shards, mesh=mesh, in_specs=placed, out_specs=P(("blk", "rel"), None), check_vma=False
    )
```

profile of v0, /device:TPU:0, one launch (start us, length us, event | category | flops | bytes accessed | tf_op | source)
XLA Modules:
  0.0 170.1 jit_solution(18058495546422584133)
XLA Ops:
  6.5 0.0 copy-start
  6.5 0.0 all-gather.3.cloned.1.call-start
  6.5 0.7 all-gather.3.cloned.1.call-update
  7.3 0.0 all-gather.5.cloned.1.call-start
  7.3 0.7 all-gather.5.cloned.1.call-update
  8.0 0.0 reduce-scatter.2.cloned.1.call-start
  8.1 0.1 shift_right_arithmetic.32
  8.1 0.8 broadcast_in_dim.14
  9.0 1.1 copy.15
  10.1 5.3 %fusion = bf16[6,512,1024]{2,1,0:T(8,128)(2,1)} fusion(s32[6,4,1024]{2,1,0:T(4,128)S(1)} %reshape.30, s32[512]{0:T(512)S(1)} %shift_right_arithmetic.32, s32[6,16,1024]{2,1,0:T(8,128)S(1)} %bitcast.37), kind=kLoop, calls=%fused_computation.1 | loop fusion | flops 12582912 | bytes 6785024 | tf_op jit(solution)/shard_map/convert_element_type | solution.py:40
  15.3 77.1 %all-gather.3.cloned.1.call-done = bf16[512,8,512]{2,1,0:T(8,128)(2,1)} async-done(((bf16[128,8,512]{2,1,0:T(8,128)(2,1)}), bf16[512,8,512]{2,1,0:T(8,128)(2,1)}) %all-gather.3.cloned.1.call-update) | async-done | bytes 4194320 | tf_op jit(solution)/shard_map/all_gather | solution.py:24
  92.4 0.0 copy-done
  92.4 7.7 %convert_bitcast_fusion = bf16[512,6,512]{2,1,0:T(8,128)(2,1)} fusion(bf16[512,8,512]{2,1,0:T(8,128)(2,1)} %all-gather.3.cloned.1.call-done, f32[6,8]{1,0:T(8,128)S(1)} %copy-done), kind=kOutput, calls=%fused_computation.6 | convolution fusion | flops 152567808 | bytes 7340224 | tf_op jit(solution)/shard_map/rb,ibj->irj/dot_general | solution.py:27
  100.1 0.0 slice-start
  100.1 7.4 %copy.10 = bf16[512,6,512]{0,2,1:T(8,128)(2,1)} copy(bf16[512,6,512]{2,1,0:T(8,128)(2,1)} %convert_bitcast_fusion) | data formatting | bytes 6291456 | tf_op jit(solution)/shard_map/convert_element_type | solution.py:29
  107.4 8.7 %all-gather.5.cloned.1.call-done = bf16[1024,512]{1,0:T(8,128)(2,1)} async-done(((bf16[128,512]{1,0:T(8,128)(2,1)}), bf16[1024,512]{1,0:T(8,128)(2,1)}) %all-gather.5.cloned.1.call-update) | async-done | bytes 1048592 | tf_op jit(solution)/shard_map/all_gather | solution.py:35
  116.2 0.0 slice-start.1
  116.2 5.8 %convolution_convert_fusion = bf16[3072,1024]{1,0:T(8,128)(2,1)S(1)} fusion(bf16[512,3072]{0,1:T(8,128)(2,1)} %bitcast.39, bf16[1024,512]{1,0:T(8,128)(2,1)} %all-gather.5.cloned.1.call-done), kind=kOutput, calls=%fused_computation.5 | convolution fusion | flops 3224371200 | bytes 10485760 | tf_op jit(solution)/shard_map/dot_general | solution.py:36
  122.0 0.0 slice-done
  122.0 0.0 slice-done.1
  122.0 0.0 copy-start.3
  122.0 0.0 copy-start.2
  122.0 0.0 copy-start.1
  122.0 4.4 %convolution_bitcast_fusion = f32[512,512]{1,0:T(8,128)} fusion(bf16[6,512,1024]{2,1,0:T(8,128)(2,1)S(1)} %bitcast.36, bf16[1024,6,512]{0,2,1:T(8,128)(2,1)S(1)} %bitcast.41), kind=kOutput, calls=%fused_computation.7 | convolution fusion | flops 3221225472 | bytes 13631488 | tf_op jit(solution)/shard_map/rns,srd->nd/dot_general | solution.py:41
  126.4 0.0 reduce-scatter.2.cloned.1.call-update
  126.5 0.1 broadcast_in_dim.16
  126.6 0.1 broadcast_in_dim.17
  126.7 2.3 %multiply_reduce_fusion = s32[16,32]{1,0:T(8,128)S(1)} fusion(s32[6,16,1024]{2,1,0:T(8,128)S(1)} %broadcast_in_dim.17, s32[6,16,1024]{2,1,0:T(8,128)S(1)} %bitcast.38), kind=kLoop, calls=%fused_computation.4 | loop fusion | flops 12582400 | bytes 788480 | tf_op jit(solution)/shard_map/reduce_sum | solution.py:39
  129.0 0.1 convert_element_type.31
  129.1 0.0 copy-done.3
  129.1 0.6 dynamic-slice
  130.3 12.2 %all-reduce = f32[512]{0:T(512)S(1)} all-reduce(f32[512]{0:T(512)S(1)} %convert_element_type.31), channel_id=3, replica_groups=mesh['blk'=8,'rel'=4] {'rel'}, use_global_device_ids=true, to_apply=%region_2.0.clone | all-reduce | flops 512 | bytes 4096
  142.5 0.1 fusion.5
  142.6 0.0 copy-done.2
  142.6 19.1 %all_gather.9 = bf16[512,512]{1,0:T(8,128)(2,1)S(1)} all-gather(bf16[128,512]{1,0:T(8,128)(2,1)S(1)} %copy-done.2), channel_id=1, replica_groups=mesh['blk'=8,'rel'=4] {'rel'}, dimensions={0}, use_global_device_ids=true | all-gather | bytes 655360 | tf_op jit(solution)/shard_map/all_gather | solution.py:25
  161.7 0.0 reduce-scatter.2.cloned.1.call-done
  161.7 0.0 copy-done.1
  161.7 1.8 %fusion.3 = bf16[128,512]{1,0:T(8,128)(2,1)} fusion(bf16[128,512]{1,0:T(8,128)(2,1)S(1)} %copy-done.1, bf16[512,512]{1,0:T(8,128)(2,1)S(1)} %all_gather.9, f32[128,512]{1,0:T(8,128)} %reduce-scatter.2.cloned.1.call-done, f32[128]{0:T(128)S(1)} %fusion.5), kind=kOutput, calls=%fused_computation.10 | convolution fusion | flops 67371008 | bytes 1049088 | tf_op jit(solution)/shard_map/dot_general | solution.py:47
  (4 shorter events, 0.0 us)
Async XLA Ops:
  6.5 85.9 %copy-start = (f32[6,8]{1,0:T(8,128)S(1)}, f32[6,8]{1,0:T(8,128)}, u32[]{:S(2)}) copy-start(f32[6,8]{1,0:T(8,128)} %param.10) | copy-start | bytes 580
  6.5 85.9 %all-gather.3.cloned.1.call-start = ((), (), s32[]{:S(2)}) async-start(), calls=%async_computation.1 | async-start | bytes 5242880 | tf_op jit(solution)/shard_map/all_gather | solution.py:24
  7.3 108.9 %all-gather.5.cloned.1.call-start = ((), (), s32[]{:S(2)}) async-start(), calls=%async_computation.2 | async-start | bytes 1179648 | tf_op jit(solution)/shard_map/all_gather | solution.py:35
  8.0 153.7 %reduce-scatter.2.cloned.1.call-start = ((), (), s32[]{:S(2)}) async-start(), calls=%async_computation.3 | async-start | bytes 1310720 | tf_op jit(solution)/shard_map/reduce_scatter | solution.py:44
  100.1 21.9 %slice-start = ((s8[6291456]{0:T(1024)(128)(4,1)}), s8[2097152]{0:T(1024)(128)(4,1)S(1)}, s32[]{:S(2)}) async-start(s8[6291456]{0:T(1024)(128)(4,1)} %bitcast.35), calls=%async_computation.4 | async-start | bytes 4194304
  116.2 5.8 %slice-start.1 = ((s8[6291456]{0:T(1024)(128)(4,1)}), s8[4194304]{0:T(1024)(128)(4,1)S(1)}, s32[]{:S(2)}) async-start(s8[6291456]{0:T(1024)(128)(4,1)} %bitcast.35), calls=%async_computation.5 | async-start | bytes 8388608
  122.0 7.1 %copy-start.3 = (u32[32]{0:T(128)S(1)}, u32[32]{0:T(128)}, u32[]{:S(2)}) copy-start(u32[32]{0:T(128)} %constant.13) | copy-start | bytes 388
  122.0 20.6 %copy-start.2 = (bf16[128,512]{1,0:T(8,128)(2,1)S(1)}, bf16[128,512]{1,0:T(8,128)(2,1)}, u32[]{:S(2)}) copy-start(bf16[128,512]{1,0:T(8,128)(2,1)} %param.11) | copy-start | bytes 393220
  122.0 39.7 %copy-start.1 = (bf16[128,512]{1,0:T(8,128)(2,1)S(1)}, bf16[128,512]{1,0:T(8,128)(2,1)}, u32[]{:S(2)}) copy-start(bf16[128,512]{1,0:T(8,128)(2,1)} %param.6) | copy-start | bytes 393220
Sparse Core Ops, SparseCore 0:
  8.9 83.4 all-gather.2
  94.3 21.8 all-gather.4
  126.6 33.5 reduce-scatter.1
where the time goes:
time: 170 us
  waiting for transfers between devices  87.2 us (51%)
  blocking collectives  31.3 us (18%)
  matrix products  19.7 us (12%)
  between operations  13.9 us (8%)
  local copies, waits for them, and re-layouts  10.3 us (6%)
  other arithmetic  7.61 us (4%)
    all_gather x1, waiting for transfers between devices, shards(): lax.all_gather(bases, 'rel', axis=0, tiled=True)  77.1 us
    all_gather x1, blocking collectives, shards(): lax.all_gather(self_weight, 'rel', axis=0, tiled=True)  19.1 us
    unnamed x1, blocking collectives  12.2 us
    all_gather x1, waiting for transfers between devices, shards(): portion = lax.all_gather(features, 'blk', axis=0, tiled=True)  8.74 us
    dot_general x1, matrix products, shards(): jnp.einsum('rb,ibj->irj', coefficients, full_bases.astype(jnp.float32), p...  7.68 us
    convert_element_type x1, local copies, waits for them, and re-layouts, shards(): rel_weight = jnp.einsum('rb,ibj->irj', coefficients, full_bases.astype(jn...  7.35 us
    dot_general x1, matrix products, shards(): jnp.dot(portion, weight_all, preferred_element_type=jnp.float32)  5.79 us
    convert_element_type x1, other arithmetic, shards(): edges = edges.astype(jnp.bfloat16)  5.27 us
  transfers between devices with their start and end apart: 3, of which 2 were waited for; matrix products, arithmetic and copies ran while one was open for 15% of the time, Pallas kernels for 0%

commit v1 on v0

v1 whole, which is shorter than its diff:
```python
import functools

import jax
import jax.numpy as jnp
from jax import lax
from jax.experimental import pallas as pl
from jax.experimental.pallas import tpu as pltpu
from jax.sharding import PartitionSpec as P

MESH = pl.DeviceIdType.MESH
GROUP = 8
CORE, NEAR, FAR = 1, 2, 4
LANES = 128


def kernel(
    n_blk, n_rel,
    feat, adj, w0_own, w1_own, out,
    f_all, e_all, a_buf, w0, w1, acc, m_send, m_recv, d_send, d_recv,
    s1_ss, s1_rs, f0_ss, f0_rs, f_ss, f_rs, w_ss, w_rs, d_ss, d_rs, m_ss, m_rs,
):
    rels, words, sources = adj.shape
    sub, width = feat.shape
    half = sub // 2
    clusters = n_blk // GROUP
    columns = width // 2
    b, j = lax.axis_index("blk"), lax.axis_index("rel")
    q, g = lax.div(b, GROUP), lax.rem(b, GROUP)

    def flip(mask):
        index = g
        for bit in (CORE, NEAR, FAR):
            if mask & bit:
                index = index + bit * (1 - 2 * lax.rem(lax.div(g, bit), 2))
        return index

    def rel_to(d):
        return lax.rem(j + d, n_rel)

    def rel_from(d):
        return lax.rem(j + n_rel - d, n_rel)

    def copy(src, dst, ss, rs, **to):
        return pltpu.make_async_remote_copy(
            src_ref=src, dst_ref=dst, send_sem=ss, recv_sem=rs, device_id=to, device_id_type=MESH
        )

    sent = []

    def send(*args, **to):
        c = copy(*args, **to)
        c.start()
        sent.append(c)

    def arrive(dst, ss, rs):
        copy(dst, dst, ss, rs, rel=rel_to(1)).wait_recv()

    def peer(mask):
        return q * GROUP + flip(mask)

    class Item:
        def __init__(self, own, slot, ss, rs, first):
            self.own, self.slot, self.ss, self.rs = own, slot, ss, rs
            self.first, self.second = first, (NEAR + FAR) - first

        def push(self, src, origin, to):
            m = origin ^ to
            send(src, self.slot(flip(origin)), self.ss(m), self.rs(m), blk=peer(to))

        def got(self, origin):
            arrive(self.slot(flip(origin)), self.ss(origin), self.rs(origin))

        def start(self):
            for to in (self.first, self.second, CORE):
                self.push(self.own, 0, to)

        def on_first(self):
            self.got(self.first)
            for to in (self.second, CORE):
                self.push(self.slot(flip(self.first)), self.first, to)

        def on_second(self):
            self.got(self.second)
            self.push(self.slot(flip(self.second)), self.second, CORE)

        def on_both(self):
            m = NEAR + FAR
            self.got(m)
            self.push(self.slot(flip(m)), m, CORE)

        def on_core(self):
            for m in (1, 3, 5, 7):
                self.got(m)

    f_items = []
    for d in range(clusters):
        origin = lax.rem(q + clusters - d, clusters)
        for h in range(2):
            i = d * 2 + h
            own = feat.at[pl.ds(h * half, half)] if d == 0 else f_all.at[origin * GROUP + g, h]
            f_items.append(Item(
                own, lambda k, origin=origin, h=h: f_all.at[origin * GROUP + k, h],
                lambda m, i=i: f_ss.at[i, m], lambda m, i=i: f_rs.at[i, m], FAR if h == 0 else NEAR,
            ))
    w_items = []
    for cg, w in enumerate((w0, w1)):
        for d in range(1, n_rel):
            i = cg * (n_rel - 1) + d - 1
            origin = rel_from(d)
            w_items.append(Item(
                w.at[origin, g], lambda k, w=w, origin=origin: w.at[origin, k],
                lambda m, i=i: w_ss.at[i, m], lambda m, i=i: w_rs.at[i, m], FAR if i % 2 == 0 else NEAR,
            ))
    half_items = (w_items[: n_rel - 1], w_items[n_rel - 1 :])

    barrier = pltpu.get_barrier_semaphore()
    for m in (CORE, NEAR, FAR):
        pl.semaphore_signal(barrier, inc=1, device_id={"blk": peer(m)}, device_id_type=MESH)
    for d in range(1, clusters):
        pl.semaphore_signal(
            barrier, inc=1, device_id={"blk": lax.rem(q + d, clusters) * GROUP + g}, device_id_type=MESH
        )
    for d in range(1, n_rel):
        pl.semaphore_signal(barrier, inc=1, device_id={"rel": rel_to(d)}, device_id_type=MESH)
    pl.semaphore_wait(barrier, 3 + (clusters - 1) + (n_rel - 1))

    def weights_out(cg):
        src, dst = ((w0_own, w0), (w1_own, w1))[cg]
        for d in range(1, n_rel):
            send(src.at[g], dst.at[j, g], s1_ss.at[cg, d - 1], s1_rs.at[cg, d - 1], rel=rel_to(d))

    def weights_in(cg, d):
        dst = (w0, w1)[cg]
        arrive(dst.at[rel_from(d), g], s1_ss.at[cg, d - 1], s1_rs.at[cg, d - 1])
        half_items[cg][d - 1].start()

    for item in f_items[:2]:
        item.start()
    weights_out(0)
    for d in range(1, clusters):
        for h in range(2):
            send(
                feat.at[pl.ds(h * half, half)], f_all.at[b, h], f0_ss.at[d, h], f0_rs.at[d, h],
                blk=lax.rem(q + d, clusters) * GROUP + g,
            )
    weights_out(1)

    f_all[b] = feat[...].reshape(2, half, width)
    w0[j] = w0_own[...]
    w1[j] = w1_own[...]
    bit = lax.broadcasted_iota(jnp.int32, (32, sources), 0)

    def unpack(r, first):
        for word in range(words):
            e = jnp.bitwise_and(jnp.right_shift(adj[r, pl.ds(word, 1), :], bit), 1).astype(jnp.float32)
            e_all[r, pl.ds(word * 32, 32), :] = e.astype(jnp.bfloat16)
            lanes = e[:, :LANES]
            for t in range(1, sources // LANES):
                lanes = lanes + e[:, t * LANES : (t + 1) * LANES]
            rows = pl.ds(word * 32, 32)
            if first:
                acc[rows, :LANES] = lanes
            else:
                acc[rows, :LANES] += lanes

    unpack(0, True)
    for r in range(1, 2):
        unpack(r, False)
    for d in range(1, clusters):
        for h in range(2):
            i = d * 2 + h
            arrive(f_all.at[lax.rem(q + clusters - d, clusters) * GROUP + g, h], f0_ss.at[d, h], f0_rs.at[d, h])
            f_items[i].start()
    for item in f_items:
        item.on_first()
    for d in range(1, n_rel):
        weights_in(0, d)
    for r in range(2, 4):
        unpack(r, False)
    for item in f_items:
        item.on_second()
    for item in f_items:
        item.on_both()
    for r in range(4, rels):
        unpack(r, False)
    d_send[...] = acc[:, :LANES].reshape(n_rel, sub, LANES).astype(jnp.bfloat16)
    for d in range(1, n_rel):
        send(d_send.at[rel_to(d)], d_recv.at[d - 1], d_ss.at[d - 1], d_rs.at[d - 1], rel=rel_to(d))
    for item in f_items:
        item.on_core()

    todo = []
    for item in half_items[0]:
        todo.append((item.on_first, item.on_second))
    for d, item in enumerate(half_items[0]):
        todo.append((item.on_both, functools.partial(weights_in, 1, d + 1)))
    per_step = -(-len(todo) // rels)
    f_flat = f_all[...].reshape(sources, width)
    for r in range(rels):
        a_buf[:, r * width : (r + 1) * width] = jnp.dot(
            e_all[r], f_flat, preferred_element_type=jnp.float32
        ).astype(jnp.bfloat16)
        for group in todo[r * per_step : (r + 1) * per_step]:
            for act in group:
                act()
    for item in half_items[1]:
        item.on_first()
    for item in half_items[1]:
        item.on_second()
    for item in half_items[0]:
        item.on_core()

    def weight_of(cg, r):
        w, per = ((w0, rels * 4 // GROUP), (w1, rels * 4 // GROUP))[cg]
        blocks = []
        for cb in range(2):
            rows = []
            for jj in range(n_rel):
                for h in range(2):
                    u = (r * 2 + cb) * 2 + h
                    rows.append(w[jj, u // per, u % per])
            blocks.append(jnp.concatenate(rows, axis=0))
        return jnp.concatenate(blocks, axis=1)

    def message(cg):
        total = None
        for r in range(rels):
            part = jnp.dot(
                a_buf[:, r * width : (r + 1) * width], weight_of(cg, r), preferred_element_type=jnp.float32
            )
            total = part if total is None else total + part
        cols = slice(cg * columns, (cg + 1) * columns)
        acc[:, cols] = total
        m_send[cg] = total.astype(jnp.bfloat16).reshape(n_rel, sub, columns)
        for d in range(1, n_rel):
            send(
                m_send.at[cg, rel_to(d)], m_recv.at[cg, d - 1], m_ss.at[cg, d - 1], m_rs.at[cg, d - 1],
                rel=rel_to(d),
            )

    message(0)
    for item in half_items[1]:
        item.on_both()
    for item in half_items[1]:
        item.on_core()
    message(1)

    per = rels * 4 // GROUP
    blocks = []
    for cb in range(4):
        rows = []
        for jj in range(n_rel):
            for h in range(2):
                rows.append(w1[jj, cb * 2 + h, per])
        blocks.append(jnp.concatenate(rows, axis=0))
    own = jnp.dot(feat[...], jnp.concatenate(blocks, axis=1), preferred_element_type=jnp.float32)
    degree = d_send[j].astype(jnp.float32)
    for d in range(1, n_rel):
        arrive(d_recv.at[d - 1], d_ss.at[d - 1], d_rs.at[d - 1])
        degree = degree + d_recv[d - 1].astype(jnp.float32)
    scale = lax.rsqrt(1.0 + jnp.sum(degree, axis=1, keepdims=True))
    for cg in range(2):
        cols = slice(cg * columns, (cg + 1) * columns)
        total = acc[pl.ds(pl.multiple_of(j * sub, sub), sub), cols]
        for d in range(1, n_rel):
            arrive(m_recv.at[cg, d - 1], m_ss.at[cg, d - 1], m_rs.at[cg, d - 1])
            total = total + m_recv[cg, d - 1].astype(jnp.float32)
        out[:, cols] = jnp.maximum(own[:, cols] + total * scale, 0.0).astype(jnp.bfloat16)
    for c in sent:
        c.wait_send()


def shards(n_blk, n_rel, features, adjacency, tile_mask, bases, coefficients, self_weight):
    rels, words = adjacency.shape[:2]
    sub, width = features.shape
    rows = bases.shape[0]
    half = rows // 2
    per = rels * 4 // GROUP
    flags = jnp.repeat(
        jnp.repeat(tile_mask.reshape(rels, tile_mask.shape[1], n_blk), words // tile_mask.shape[1], axis=1), sub, axis=2
    )
    masked = jnp.bitwise_and(adjacency.reshape(rels, words, n_blk * sub), -flags)
    weight = jnp.einsum(
        "rb,ibj->rij", coefficients, bases.astype(jnp.float32), precision=lax.Precision.HIGHEST
    ).astype(jnp.bfloat16)
    units = weight.reshape(rels, 2, half, 2, 2, LANES).transpose(3, 0, 4, 1, 2, 5)
    units = units.reshape(2, GROUP, per, half, LANES)
    self_units = self_weight.reshape(2, half, 4, LANES).transpose(2, 0, 1, 3).reshape(GROUP, 1, half, LANES)
    w1_own = jnp.concatenate([units[1], self_units], axis=1)
    dests = words * 32
    clusters = n_blk // GROUP
    bf, dma = jnp.bfloat16, pltpu.SemaphoreType.DMA
    links = n_rel - 1
    vmem = pl.BlockSpec(memory_space=pltpu.VMEM)
    return pl.pallas_call(
        functools.partial(kernel, n_blk, n_rel),
        out_shape=jax.ShapeDtypeStruct((sub, width), bf),
        in_specs=[vmem] * 4,
        out_specs=vmem,
        scratch_shapes=[
            pltpu.VMEM((n_blk, 2, sub // 2, width), bf),
            pltpu.VMEM((rels, dests, n_blk * sub), bf),
            pltpu.VMEM((dests, rels * width), bf),
            pltpu.VMEM((n_rel, GROUP, per, half, LANES), bf),
            pltpu.VMEM((n_rel, GROUP, per + 1, half, LANES), bf),
            pltpu.VMEM((dests, width), jnp.float32),
            pltpu.VMEM((2, n_rel, sub, width // 2), bf),
            pltpu.VMEM((2, links, sub, width // 2), bf),
            pltpu.VMEM((n_rel, sub, LANES), bf),
            pltpu.VMEM((links, sub, LANES), bf),
            dma((2, links)), dma((2, links)),
            dma((clusters, 2)), dma((clusters, 2)),
            dma((clusters * 2, GROUP)), dma((clusters * 2, GROUP)),
            dma((2 * links, GROUP)), dma((2 * links, GROUP)),
            dma((links,)), dma((links,)),
            dma((2, links)), dma((2, links)),
        ],
        compiler_params=pltpu.CompilerParams(
            collective_id=0, has_side_effects=True, vmem_limit_bytes=48 * 1024 * 1024
        ),
    )(features, masked, units[0], w1_own)


def solution(mesh):
    n_blk, n_rel = mesh.shape["blk"], mesh.shape["rel"]
    placed = (
        P(("blk", "rel"), None),
        P(None, "blk", "rel", None),
        P(None, "blk", None, "rel"),
        P("rel", None, None),
        P(),
        P("rel", None),
    )
    return jax.shard_map(
        functools.partial(shards, n_blk, n_rel),
        mesh=mesh, in_specs=placed, out_specs=P(("blk", "rel"), None), check_vma=False,
    )
```

time: 170 us -> 49.1 us (0.29)
  waiting for transfers between devices: 87.2 us -> 0 us
  Pallas kernels: 0 us -> 41.3 us
  blocking collectives: 31.3 us -> 0 us
  matrix products: 19.7 us -> 1.65 us
  between operations: 13.9 us -> 0.14 us
  other arithmetic: 7.61 us -> 0.16 us
  local copies, waits for them, and re-layouts: 10.3 us -> 5.53 us
    all_gather x2 -> x0, waiting for transfers between devices: 85.8 us -> none  [the longest x1 77.1 us: shards(): lax.all_gather(bases, 'rel', axis=0, tiled=True)]
    pallas_call x0 -> x1, Pallas kernels: none -> 41.3 us  [shards(): pl.pallas_call(functools.partial(kernel, n_blk, n_rel), out_shape=jax.Sha...]
    all_gather x1 -> x0, blocking collectives: 19.1 us -> none  [shards(): lax.all_gather(self_weight, 'rel', axis=0, tiled=True)]
    dot_general x4 -> x1, matrix products: 19.7 us -> 1.65 us  [shards(): jnp.einsum('rb,ibj->rij', coefficients, bases.astype(jnp.float32), precis...]
    unnamed x1 -> x0, blocking collectives: 12.2 us -> none
    convert_element_type x2 -> x0, local copies, waits for them, and re-layouts: 7.43 us -> none  [the longest x1 7.35 us: shards(): rel_weight = jnp.einsum('rb,ibj->irj', coefficients, full_bases.astype(jn...]
    convert_element_type x2 -> x0, other arithmetic: 5.27 us -> none  [the longest x1 5.27 us: shards(): edges = edges.astype(jnp.bfloat16)]
    reduce_sum x1 -> x0, other arithmetic: 2.26 us -> none  [shards(): degree = jnp.sum(edges, axis=(0, 2)).astype(jnp.float32)]
  transfers between devices with their start and end apart: 3 -> 0, of which waited for: 2 -> 0; matrix products, arithmetic and copies ran while one was open for 15% -> 0% of each run, Pallas kernels for 0% -> 0%
where the time goes in v1:
time: 49.1 us; the launch traced here: 48.8 us
  Pallas kernels  41.3 us (84%)
  local copies, waits for them, and re-layouts  5.53 us (11%)
  matrix products  1.65 us (3%)
    pallas_call x1, Pallas kernels, shards(): pl.pallas_call(functools.partial(kernel, n_blk, n_rel), out_shape=jax.Sha...  41.3 us
    unnamed x11, local copies, waits for them, and re-layouts  3.18 us
    dot_general x1, matrix products, shards(): jnp.einsum('rb,ibj->rij', coefficients, bases.astype(jnp.float32), precis...  1.65 us
    reshape x2, local copies, waits for them, and re-layouts, shards(): weight.reshape(rels, 2, half, 2, 2, LANES).transpose(3, 0, 4, 1, 2, 5)  1.1 us

profile of v1, /device:TPU:0, one launch (start us, length us, event | category | flops | bytes accessed | tf_op | source)
XLA Modules:
  0.0 48.8 jit_solution(17984162075573353369)
XLA Ops:
  0.0 0.0 copy-start
  0.0 1.2 %copy-done = bf16[128,8,512]{2,1,0:T(8,128)(2,1)S(1)} copy-done((bf16[128,8,512]{2,1,0:T(8,128)(2,1)S(1)}, bf16[128,8,512]{2,1,0:T(8,128)(2,1)}, u32[]{:S(2)}) %copy-start) | copy-done | bytes 1048600
  1.2 1.6 %convolution_convert_fusion = bf16[6,128,512]{2,0,1:T(8,128)(2,1)S(1)} fusion(bf16[128,8,512]{2,1,0:T(8,128)(2,1)S(1)} %copy-done, f32[6,8]{1,0:T(8,128)} %param.10), kind=kOutput, calls=%fused_computation | convolution fusion | flops 38141952 | bytes 1835200 | tf_op jit(solution)/shard_map/rb,ibj->rij/dot_general | solution.py:283
  2.9 0.4 reshape.28
  3.3 0.7 %copy.17 = bf16[6,2,64,2,2,128]{5,4,3,2,1,0:T(2,128)(2,1)S(1)} copy(bf16[6,2,64,2,2,128]{5,4,3,0,2,1:T(2,128)(2,1)S(1)} %reshape.28) | data formatting | bytes 1572864 | tf_op jit(solution)/shard_map/reshape | solution.py:286
  4.0 0.0 copy-start.3
  4.0 0.8 %fusion.1 = (bf16[1,6,2,2,64,128]{5,2,0,4,3,1:T(2,128)(2,1)S(1)}, bf16[1,6,2,2,64,128]{5,2,0,4,3,1:T(2,128)(2,1)S(1)}) fusion(bf16[2,6,2,2,64,128]{5,2,0,4,3,1:T(2,128)(2,1)S(1)} %bitcast.21), kind=kLoop, calls=%fused_computation.5 | loop fusion | bytes 1572864 | tf_op jit(solution)/shard_map/slice | solution.py:289
  4.8 0.1 copy.11
  4.9 0.0 copy-done.3
  5.0 0.0 copy-start.4
  5.0 0.1 pad_maximum_fusion.w1_own
  5.0 0.0 copy-start.2
  5.1 0.1 copy.10
  5.1 0.5 %copy-done.4 = s32[6,4,8,1]{2,3,1,0:T(1,128)S(1)} copy-done((s32[6,4,8,1]{2,3,1,0:T(1,128)S(1)}, s32[6,4,8,1]{2,3,1,0:T(1,128)}, u32[]{:S(2)}) %copy-start.4) | copy-done | bytes 792
  5.7 0.2 broadcast_in_dim.7
  5.9 0.0 copy-start.1
  5.9 0.1 neg.17
  5.9 0.1 copy-done.2
  6.0 0.1 bitcast_and_fusion.adj
  6.1 0.7 %copy-done.1 = bf16[128,512]{1,0:T(8,128)(2,1)S(1)} copy-done((bf16[128,512]{1,0:T(8,128)(2,1)S(1)}, bf16[128,512]{1,0:T(8,128)(2,1)}, u32[]{:S(2)}) %copy-start.1) | copy-done | bytes 131096
  6.8 41.3 %shard_map.64 = bf16[128,512]{1,0:T(8,128)(2,1)S(1)} custom-call(bf16[128,512]{1,0:T(8,128)(2,1)S(1)} %copy-done.1, s32[6,16,1024]{2,1,0:T(8,128)S(1)} %bitcast_and_fusion.adj, bf16[8,3,64,128]{3,2,1,0:T(8,128)(2,1)S(1)} %bitcast.20, bf16[8,4,64,128]{3,2,1,0:T(8,128)(2,1)S(1)} %pad_maximum_fusion.w1_own), custom_call_target="tpu_custom_call" | custom-call | tf_op jit(solution)/shard_map/pallas_call | solution.py:295
  48.1 0.7 %copy.19 = bf16[128,512]{1,0:T(8,128)(2,1)} copy(bf16[128,512]{1,0:T(8,128)(2,1)S(1)} %shard_map.64) | data formatting | bytes 262144
  (4 shorter events, 0.1 us)
Async XLA Ops:
  0.0 1.2 %copy-start = (bf16[128,8,512]{2,1,0:T(8,128)(2,1)S(1)}, bf16[128,8,512]{2,1,0:T(8,128)(2,1)}, u32[]{:S(2)}) copy-start(bf16[128,8,512]{2,1,0:T(8,128)(2,1)} %param.9) | copy-start | bytes 3145732
  4.0 0.9 %copy-start.3 = (bf16[128,512]{1,0:T(8,128)(2,1)S(1)}, bf16[128,512]{1,0:T(8,128)(2,1)}, u32[]{:S(2)}) copy-start(bf16[128,512]{1,0:T(8,128)(2,1)} %param.11) | copy-start | bytes 393220
  5.0 0.7 %copy-start.4 = (s32[6,4,8,1]{2,3,1,0:T(1,128)S(1)}, s32[6,4,8,1]{2,3,1,0:T(1,128)}, u32[]{:S(2)}) copy-start(s32[6,4,8,1]{2,3,1,0:T(1,128)} %param.8) | copy-start | bytes 2308
  5.0 1.0 %copy-start.2 = (s32[6,16,1,1024]{3,2,1,0:T(1,128)S(1)}, s32[6,16,1,1024]{3,2,1,0:T(1,128)}, u32[]{:S(2)}) copy-start(s32[6,16,1,1024]{3,2,1,0:T(1,128)} %param.7) | copy-start | bytes 1179652
  5.9 0.9 %copy-start.1 = (bf16[128,512]{1,0:T(8,128)(2,1)S(1)}, bf16[128,512]{1,0:T(8,128)(2,1)}, u32[]{:S(2)}) copy-start(bf16[128,512]{1,0:T(8,128)(2,1)} %feat.1) | copy-start | bytes 393220

commit v2 on v1

--- a/solution.py
+++ b/solution.py
@@ -14,16 +14,25 @@
 
 
 def kernel(
-    n_blk, n_rel,
-    feat, adj, w0_own, w1_own, out,
-    f_all, e_all, a_buf, w0, w1, acc, m_send, m_recv, d_send, d_recv,
-    s1_ss, s1_rs, f0_ss, f0_rs, f_ss, f_rs, w_ss, w_rs, d_ss, d_rs, m_ss, m_rs,
+    n_blk, n_rel, plan,
+    feat, adj_hbm, flags, bases_hbm, coef, self_hbm, out,
+    adj, bases, self_w, f_all, e_all, a_buf, acc, d_send, d_recv,
+    in_sem, s1_ss, s1_rs, f0_ss, f0_rs, f_ss, f_rs, w_ss, w_rs, d_ss, d_rs, m_ss, m_rs, *grouped,
 ):
+    pieces, groups = plan
+    weights, m_send, m_recv = (grouped[k * len(groups) : (k + 1) * len(groups)] for k in range(3))
+    loads = [
+        pltpu.make_async_copy(src, dst, in_sem.at[k])
+        for k, (src, dst) in enumerate(((bases_hbm, bases), (self_hbm, self_w), (adj_hbm, adj)))
+    ]
+    for load in loads:
+        load.start()
     rels, words, sources = adj.shape
     sub, width = feat.shape
+    pers = [rels * len(cbs) * pieces // GROUP for cbs in groups]
+    self_per = width // LANES * pieces // GROUP
     half = sub // 2
     clusters = n_blk // GROUP
-    columns = width // 2
     b, j = lax.axis_index("blk"), lax.axis_index("rel")
     q, g = lax.div(b, GROUP), lax.rem(b, GROUP)
 
@@ -71,7 +80,14 @@
             arrive(self.slot(flip(origin)), self.ss(origin), self.rs(origin))
 
         def start(self):
-            for to in (self.first, self.second, CORE):
+            self.start_first()
+            self.start_rest()
+
+        def start_first(self):
+            self.push(self.own, 0, self.first)
+
+        def start_rest(self):
+            for to in (self.second, CORE):
                 self.push(self.own, 0, to)
 
         def on_first(self):
@@ -103,7 +119,7 @@
                 lambda m, i=i: f_ss.at[i, m], lambda m, i=i: f_rs.at[i, m], FAR if h == 0 else NEAR,
             ))
     w_items = []
-    for cg, w in enumerate((w0, w1)):
+    for cg, w in enumerate(weights):
         for d in range(1, n_rel):
             i = cg * (n_rel - 1) + d - 1
             origin = rel_from(d)
@@ -111,7 +127,7 @@
                 w.at[origin, g], lambda k, w=w, origin=origin: w.at[origin, k],
                 lambda m, i=i: w_ss.at[i, m], lambda m, i=i: w_rs.at[i, m], FAR if i % 2 == 0 else NEAR,
             ))
-    half_items = (w_items[: n_rel - 1], w_items[n_rel - 1 :])
+    group_items = [w_items[k * (n_rel - 1) : (k + 1) * (n_rel - 1)] for k in range(len(groups))]
 
     barrier = pltpu.get_barrier_semaphore()
     for m in (CORE, NEAR, FAR):
@@ -125,34 +141,82 @@
     pl.semaphore_wait(barrier, 3 + (clusters - 1) + (n_rel - 1))
 
     def weights_out(cg):
-        src, dst = ((w0_own, w0), (w1_own, w1))[cg]
+        w = weights[cg]
         for d in range(1, n_rel):
-            send(src.at[g], dst.at[j, g], s1_ss.at[cg, d - 1], s1_rs.at[cg, d - 1], rel=rel_to(d))
+            send(w.at[j, g], w.at[j, g], s1_ss.at[cg, d - 1], s1_rs.at[cg, d - 1], rel=rel_to(d))
 
     def weights_in(cg, d):
-        dst = (w0, w1)[cg]
+        dst = weights[cg]
         arrive(dst.at[rel_from(d), g], s1_ss.at[cg, d - 1], s1_rs.at[cg, d - 1])
-        half_items[cg][d - 1].start()
+        group_items[cg][d - 1].start()
 
     for item in f_items[:2]:
-        item.start()
-    weights_out(0)
+        item.start_first()
+    for item in f_items[:2]:
+        item.start_rest()
     for d in range(1, clusters):
         for h in range(2):
             send(
                 feat.at[pl.ds(h * half, half)], f_all.at[b, h], f0_ss.at[d, h], f0_rs.at[d, h],
                 blk=lax.rem(q + d, clusters) * GROUP + g,
             )
-    weights_out(1)
+
+    basis, chunk = coef.shape[1], 16
+    deep = chunk * basis
+    spread = lax.broadcasted_iota(jnp.int32, (basis, deep), 1) % basis == lax.broadcasted_iota(
+        jnp.int32, (basis, deep), 0
+    )
+    tiled = jnp.dot(
+        coef[...], spread.astype(jnp.float32), precision=lax.Precision.HIGHEST, preferred_element_type=jnp.float32
+    )
+    diagonal = lax.broadcasted_iota(jnp.int32, (chunk, deep), 1) // basis == lax.broadcasted_iota(
+        jnp.int32, (chunk, deep), 0
+    )
+    mixing = jnp.concatenate([jnp.where(diagonal, tiled[r : r + 1, :], 0.0) for r in range(rels)], axis=0)
+    high = mixing.astype(jnp.bfloat16)
+    low = (mixing - high.astype(jnp.float32)).astype(jnp.bfloat16)
+    mixing = jnp.concatenate([high, low], axis=1)
+    depth = self_w.shape[0] // pieces
+    loads[0].wait()
+    for k in range(self_w.shape[0] // chunk):
+        rows = bases[pl.ds(k * deep, deep), :]
+        made = jnp.dot(
+            mixing, jnp.concatenate([rows, rows], axis=0), preferred_element_type=jnp.float32
+        ).astype(jnp.bfloat16)
+        h, at = k * chunk // depth, k * chunk % depth
+        for cg, cbs in enumerate(groups):
+            for r in range(rels):
+                for c, cb in enumerate(cbs):
+                    u = (r * len(cbs) + c) * pieces + h
+                    weights[cg][j, u // pers[cg], u % pers[cg], at : at + chunk, :] = made[
+                        r * chunk : (r + 1) * chunk, cb * LANES : (cb + 1) * LANES
+                    ]
+    loads[1].wait()
+    for cb in range(width // LANES):
+        for h in range(pieces):
+            u = cb * pieces + h
+            weights[0][j, u // self_per, pers[0] + u % self_per] = self_w[
+                h * depth : (h + 1) * depth, cb * LANES : (cb + 1) * LANES
+            ]
+    for cg in range(len(groups)):
+        weights_out(cg)
 
     f_all[b] = feat[...].reshape(2, half, width)
-    w0[j] = w0_own[...]
-    w1[j] = w1_own[...]
+    owner = lax.broadcasted_iota(jnp.int32, (n_blk, sources), 1) // sub == lax.broadcasted_iota(
+        jnp.int32, (n_blk, sources), 0
+    )
+    keep = -jnp.dot(
+        flags[...].astype(jnp.float32), owner.astype(jnp.float32), preferred_element_type=jnp.float32
+    ).astype(jnp.int32)
+    tiles = flags.shape[0] // rels
+    loads[2].wait()
     bit = lax.broadcasted_iota(jnp.int32, (32, sources), 0)
 
     def unpack(r, first):
         for word in range(words):
-            e = jnp.bitwise_and(jnp.right_shift(adj[r, pl.ds(word, 1), :], bit), 1).astype(jnp.float32)
+            tile = r * tiles + word * tiles // words
+            masked = jnp.bitwise_and(adj[r, pl.ds(word, 1), :], keep[tile : tile + 1, :])
+            e = jnp.bitwise_and(jnp.right_shift(masked, bit), 1).astype(jnp.float32)
             e_all[r, pl.ds(word * 32, 32), :] = e.astype(jnp.bfloat16)
             lanes = e[:, :LANES]
             for t in range(1, sources // LANES):
@@ -190,9 +254,9 @@
         item.on_core()
 
     todo = []
-    for item in half_items[0]:
+    for item in group_items[0]:
         todo.append((item.on_first, item.on_second))
-    for d, item in enumerate(half_items[0]):
+    for d, item in enumerate(group_items[0]):
         todo.append((item.on_both, functools.partial(weights_in, 1, d + 1)))
     per_step = -(-len(todo) // rels)
     f_flat = f_all[...].reshape(sources, width)
@@ -203,24 +267,32 @@
         for group in todo[r * per_step : (r + 1) * per_step]:
             for act in group:
                 act()
-    for item in half_items[1]:
-        item.on_first()
-    for item in half_items[1]:
-        item.on_second()
-    for item in half_items[0]:
-        item.on_core()
+
+    def spread_group(cg):
+        for item in group_items[cg]:
+            item.on_first()
+            item.on_second()
+
+    def finish_group(cg):
+        for item in group_items[cg]:
+            item.on_both()
+        for item in group_items[cg]:
+            item.on_core()
 
     def weight_of(cg, r):
-        w, per = ((w0, rels * 4 // GROUP), (w1, rels * 4 // GROUP))[cg]
+        w, per, cbs = weights[cg], pers[cg], groups[cg]
         blocks = []
-        for cb in range(2):
+        for c in range(len(cbs)):
             rows = []
             for jj in range(n_rel):
-                for h in range(2):
-                    u = (r * 2 + cb) * 2 + h
+                for h in range(pieces):
+                    u = (r * len(cbs) + c) * pieces + h
                     rows.append(w[jj, u // per, u % per])
             blocks.append(jnp.concatenate(rows, axis=0))
         return jnp.concatenate(blocks, axis=1)
+
+    def columns_of(cg):
+        return slice(groups[cg][0] * LANES, (groups[cg][-1] + 1) * LANES)
 
     def message(cg):
         total = None
@@ -229,42 +301,51 @@
                 a_buf[:, r * width : (r + 1) * width], weight_of(cg, r), preferred_element_type=jnp.float32
             )
             total = part if total is None else total + part
-        cols = slice(cg * columns, (cg + 1) * columns)
-        acc[:, cols] = total
-        m_send[cg] = total.astype(jnp.bfloat16).reshape(n_rel, sub, columns)
+        acc[:, columns_of(cg)] = total
+        m_send[cg][...] = total.astype(jnp.bfloat16).reshape(m_send[cg].shape)
         for d in range(1, n_rel):
             send(
-                m_send.at[cg, rel_to(d)], m_recv.at[cg, d - 1], m_ss.at[cg, d - 1], m_rs.at[cg, d - 1],
+                m_send[cg].at[rel_to(d)], m_recv[cg].at[d - 1], m_ss.at[cg, d - 1], m_rs.at[cg, d - 1],
                 rel=rel_to(d),
             )
 
-    message(0)
-    for item in half_items[1]:
-        item.on_both()
-    for item in half_items[1]:
-        item.on_core()
-    message(1)
-
-    per = rels * 4 // GROUP
-    blocks = []
-    for cb in range(4):
-        rows = []
-        for jj in range(n_rel):
-            for h in range(2):
-                rows.append(w1[jj, cb * 2 + h, per])
-        blocks.append(jnp.concatenate(rows, axis=0))
-    own = jnp.dot(feat[...], jnp.concatenate(blocks, axis=1), preferred_element_type=jnp.float32)
+    def self_term():
+        blocks = []
+        for cb in range(width // LANES):
+            rows = []
+            for jj in range(n_rel):
+                for h in range(pieces):
+                    u = cb * pieces + h
+                    rows.append(weights[0][jj, u // self_per, pers[0] + u % self_per])
+            blocks.append(jnp.concatenate(rows, axis=0))
+        return jnp.dot(feat[...], jnp.concatenate(blocks, axis=1), preferred_element_type=jnp.float32)
+
+    for cg in range(1, len(groups)):
+        spread_group(cg)
+        if cg + 1 < len(groups):
+            for d in range(1, n_rel):
+                weights_in(cg + 1, d)
+        if cg == 1:
+            for item in group_items[0]:
+                item.on_core()
+        else:
+            finish_group(cg - 1)
+        message(cg - 1)
+    own = self_term()
+    finish_group(len(groups) - 1)
+    message(len(groups) - 1)
+
     degree = d_send[j].astype(jnp.float32)
     for d in range(1, n_rel):
         arrive(d_recv.at[d - 1], d_ss.at[d - 1], d_rs.at[d - 1])
         degree = degree + d_recv[d - 1].astype(jnp.float32)
     scale = lax.rsqrt(1.0 + jnp.sum(degree, axis=1, keepdims=True))
-    for cg in range(2):
-        cols = slice(cg * columns, (cg + 1) * columns)
+    for cg in range(len(groups)):
+        cols = columns_of(cg)
         total = acc[pl.ds(pl.multiple_of(j * sub, sub), sub), cols]
         for d in range(1, n_rel):
-            arrive(m_recv.at[cg, d - 1], m_ss.at[cg, d - 1], m_rs.at[cg, d - 1])
-            total = total + m_recv[cg, d - 1].astype(jnp.float32)
+            arrive(m_recv[cg].at[d - 1], m_ss.at[cg, d - 1], m_rs.at[cg, d - 1])
+            total = total + m_recv[cg][d - 1].astype(jnp.float32)
         out[:, cols] = jnp.maximum(own[:, cols] + total * scale, 0.0).astype(jnp.bfloat16)
     for c in sent:
         c.wait_send()
@@ -273,52 +354,58 @@
 def shards(n_blk, n_rel, features, adjacency, tile_mask, bases, coefficients, self_weight):
     rels, words = adjacency.shape[:2]
     sub, width = features.shape
-    rows = bases.shape[0]
-    half = rows // 2
-    per = rels * 4 // GROUP
-    flags = jnp.repeat(
-        jnp.repeat(tile_mask.reshape(rels, tile_mask.shape[1], n_blk), words // tile_mask.shape[1], axis=1), sub, axis=2
-    )
-    masked = jnp.bitwise_and(adjacency.reshape(rels, words, n_blk * sub), -flags)
-    weight = jnp.einsum(
-        "rb,ibj->rij", coefficients, bases.astype(jnp.float32), precision=lax.Precision.HIGHEST
-    ).astype(jnp.bfloat16)
-    units = weight.reshape(rels, 2, half, 2, 2, LANES).transpose(3, 0, 4, 1, 2, 5)
-    units = units.reshape(2, GROUP, per, half, LANES)
-    self_units = self_weight.reshape(2, half, 4, LANES).transpose(2, 0, 1, 3).reshape(GROUP, 1, half, LANES)
-    w1_own = jnp.concatenate([units[1], self_units], axis=1)
+    rows, basis = bases.shape[:2]
+    blocks = width // LANES
+    pieces = 4 if rows // 4 >= 16 else 2
+    if pieces == 4:
+        groups = (tuple(range(blocks // 2)), tuple(range(blocks // 2, blocks - 1)), (blocks - 1,))
+    else:
+        groups = (tuple(range(blocks // 2)), tuple(range(blocks // 2, blocks)))
+    pers = [rels * len(cbs) * pieces // GROUP for cbs in groups]
+    pers[0] += blocks * pieces // GROUP
+    depth = rows // pieces
     dests = words * 32
     clusters = n_blk // GROUP
     bf, dma = jnp.bfloat16, pltpu.SemaphoreType.DMA
-    links = n_rel - 1
-    vmem = pl.BlockSpec(memory_space=pltpu.VMEM)
+    links, parts = n_rel - 1, len(groups)
+    vmem, anywhere = pl.BlockSpec(memory_space=pltpu.VMEM), pl.BlockSpec(memory_space=pl.ANY)
     return pl.pallas_call(
-        functools.partial(kernel, n_blk, n_rel),
+        functools.partial(kernel, n_blk, n_rel, (pieces, groups)),
         out_shape=jax.ShapeDtypeStruct((sub, width), bf),
-        in_specs=[vmem] * 4,
+        in_specs=[vmem, anywhere, vmem, anywhere, vmem, anywhere],
         out_specs=vmem,
         scratch_shapes=[
+            pltpu.VMEM((rels, words, n_blk * sub), jnp.int32),
+            pltpu.VMEM((rows * basis, width), bf),
+            pltpu.VMEM((rows, width), bf),
             pltpu.VMEM((n_blk, 2, sub // 2, width), bf),
             pltpu.VMEM((rels, dests, n_blk * sub), bf),
             pltpu.VMEM((dests, rels * width), bf),
-            pltpu.VMEM((n_rel, GROUP, per, half, LANES), bf),
-            pltpu.VMEM((n_rel, GROUP, per + 1, half, LANES), bf),
             pltpu.VMEM((dests, width), jnp.float32),
-            pltpu.VMEM((2, n_rel, sub, width // 2), bf),
-            pltpu.VMEM((2, links, sub, width // 2), bf),
             pltpu.VMEM((n_rel, sub, LANES), bf),
             pltpu.VMEM((links, sub, LANES), bf),
-            dma((2, links)), dma((2, links)),
+            dma((3,)),
+            dma((parts, links)), dma((parts, links)),
             dma((clusters, 2)), dma((clusters, 2)),
             dma((clusters * 2, GROUP)), dma((clusters * 2, GROUP)),
-            dma((2 * links, GROUP)), dma((2 * links, GROUP)),
+            dma((parts * links, GROUP)), dma((parts * links, GROUP)),
             dma((links,)), dma((links,)),
-            dma((2, links)), dma((2, links)),
+            dma((parts, links)), dma((parts, links)),
+            *[pltpu.VMEM((n_rel, GROUP, per, depth, LANES), bf) for per in pers],
+            *[pltpu.VMEM((n_rel, sub, len(cbs) * LANES), bf) for cbs in groups],
+            *[pltpu.VMEM((links, sub, len(cbs) * LANES), bf) for cbs in groups],
         ],
         compiler_params=pltpu.CompilerParams(
             collective_id=0, has_side_effects=True, vmem_limit_bytes=48 * 1024 * 1024
         ),
-    )(features, masked, units[0], w1_own)
+    )(
+        features,
+        adjacency.reshape(rels, words, n_blk * sub),
+        tile_mask.reshape(rels * tile_mask.shape[1], n_blk),
+        bases.reshape(rows * basis, width),
+        coefficients,
+        self_weight,
+    )
 
 
 def solution(mesh):

time: 49.1 us -> 48.1 us (0.980)
  Pallas kernels: 41.3 us -> 44.9 us
  local copies, waits for them, and re-layouts: 5.53 us -> 3 us
  matrix products: 1.65 us -> 0 us
    pallas_call x1, Pallas kernels: 41.3 us -> 44.9 us  [shards(): pl.pallas_call(functools.partial(kernel, n_blk, n_rel, (pieces, groups)),...]
    dot_general x1 -> x0, matrix products: 1.65 us -> none  [shards(): jnp.einsum('rb,ibj->rij', coefficients, bases.astype(jnp.float32), precis...]
    reshape x4 -> x0, local copies, waits for them, and re-layouts: 1.15 us -> none  [the longest x2 1.1 us: shards(): weight.reshape(rels, 2, half, 2, 2, LANES).transpose(3, 0, 4, 1, 2, 5)]
    slice x3 -> x0, local copies, waits for them, and re-layouts: 0.96 us -> none  [the longest x2 0.88 us: shards(): w1_own = jnp.concatenate([units[1], self_units], axis=1)]
    unnamed x11 -> x12, local copies, waits for them, and re-layouts: 3.18 us -> 3 us
where the time goes in v2:
time: 48.1 us; the launch traced here: 48 us
  Pallas kernels  44.9 us (93%)
  local copies, waits for them, and re-layouts  3 us (6%)
    pallas_call x1, Pallas kernels, shards(): pl.pallas_call(functools.partial(kernel, n_blk, n_rel, (pieces, groups)),...  44.9 us
    unnamed x12, local copies, waits for them, and re-layouts  3 us

profile of v2, /device:TPU:0, one launch (start us, length us, event | category | flops | bytes accessed | tf_op | source)
XLA Modules:
  0.0 48.0 jit_solution(11339987884250956190)
XLA Ops:
  0.0 0.0 copy-start.1
  0.0 0.0 copy-start.2
  0.0 0.0 copy-start.3
  0.0 0.0 copy-start.4
  0.0 1.1 %copy.9 = s32[6,16,1,1024]{3,1,2,0:T(8,128)S(1)} copy(s32[6,16,1,1024]{3,2,1,0:T(1,128)} %param.7) | data formatting | bytes 786432
  1.1 0.0 copy-done.1
  1.1 0.0 copy-done.2
  1.1 0.0 copy-done.3
  1.2 0.0 copy-done.4
  1.2 0.0 copy-start
  1.2 1.2 %copy-done = bf16[128,8,512]{2,1,0:T(8,128)(2,1)S(1)} copy-done((bf16[128,8,512]{2,1,0:T(8,128)(2,1)S(1)}, bf16[128,8,512]{2,1,0:T(8,128)(2,1)}, u32[]{:S(2)}) %copy-start) | copy-done | bytes 1048600
  2.4 44.9 %shard_map.64 = bf16[128,512]{1,0:T(8,128)(2,1)S(1)} custom-call(bf16[128,512]{1,0:T(8,128)(2,1)S(1)} %copy-done.1, s32[6,16,1024]{2,1,0:T(8,128)S(1)} %bitcast.5, s32[24,8]{1,0:T(8,128)S(1)} %bitcast.7, bf16[1024,512]{1,0:T(8,128)(2,1)S(1)} %bitcast.6, f32[6,8]{1,0:T(8,128)S(1)} %copy-done.4, bf16[128,512]{1,0:T(8,128)(2,1)S(1)} %copy-done.2), custom_call_target="tpu_custom_call" | custom-call | tf_op jit(solution)/shard_map/pallas_call | solution.py:372
  47.3 0.7 %copy.11 = bf16[128,512]{1,0:T(8,128)(2,1)} copy(bf16[128,512]{1,0:T(8,128)(2,1)S(1)} %shard_map.64) | data formatting | bytes 262144
Async XLA Ops:
  0.0 1.1 %copy-start.1 = (bf16[128,512]{1,0:T(8,128)(2,1)S(1)}, bf16[128,512]{1,0:T(8,128)(2,1)}, u32[]{:S(2)}) copy-start(bf16[128,512]{1,0:T(8,128)(2,1)} %feat.1) | copy-start | bytes 393220
  0.0 1.1 %copy-start.2 = (bf16[128,512]{1,0:T(8,128)(2,1)S(1)}, bf16[128,512]{1,0:T(8,128)(2,1)}, u32[]{:S(2)}) copy-start(bf16[128,512]{1,0:T(8,128)(2,1)} %self_hbm.1) | copy-start | bytes 393220
  0.0 1.1 %copy-start.3 = (s32[6,4,8,1]{2,3,1,0:T(1,128)S(1)}, s32[6,4,8,1]{2,3,1,0:T(1,128)}, u32[]{:S(2)}) copy-start(s32[6,4,8,1]{2,3,1,0:T(1,128)} %param.8) | copy-start | bytes 2308
  0.0 1.1 %copy-start.4 = (f32[6,8]{1,0:T(8,128)S(1)}, f32[6,8]{1,0:T(8,128)}, u32[]{:S(2)}) copy-start(f32[6,8]{1,0:T(8,128)} %coef.1) | copy-start | bytes 580
  1.2 1.2 %copy-start = (bf16[128,8,512]{2,1,0:T(8,128)(2,1)S(1)}, bf16[128,8,512]{2,1,0:T(8,128)(2,1)}, u32[]{:S(2)}) copy-start(bf16[128,8,512]{2,1,0:T(8,128)(2,1)} %param.9) | copy-start | bytes 3145732

commit v3 on v2

--- a/solution.py
+++ b/solution.py
@@ -357,10 +357,7 @@
     rows, basis = bases.shape[:2]
     blocks = width // LANES
     pieces = 4 if rows // 4 >= 16 else 2
-    if pieces == 4:
-        groups = (tuple(range(blocks // 2)), tuple(range(blocks // 2, blocks - 1)), (blocks - 1,))
-    else:
-        groups = (tuple(range(blocks // 2)), tuple(range(blocks // 2, blocks)))
+    groups = (tuple(range(blocks // 2)), tuple(range(blocks // 2, blocks)))
     pers = [rels * len(cbs) * pieces // GROUP for cbs in groups]
     pers[0] += blocks * pieces // GROUP
     depth = rows // pieces

time: 48.1 us -> 45.1 us (0.938)
  Pallas kernels: 44.9 us -> 41.9 us
    pallas_call x1, Pallas kernels: 44.9 us -> 41.9 us  [shards(): pl.pallas_call(functools.partial(kernel, n_blk, n_rel, (pieces, groups)),...]
where the time goes in v3:
time: 45.1 us; the launch traced here: 44.9 us
  Pallas kernels  41.9 us (93%)
  local copies, waits for them, and re-layouts  3 us (7%)
    pallas_call x1, Pallas kernels, shards(): pl.pallas_call(functools.partial(kernel, n_blk, n_rel, (pieces, groups)),...  41.9 us
    unnamed x12, local copies, waits for them, and re-layouts  3 us

profile of v3, /device:TPU:0, one launch (start us, length us, event | category | flops | bytes accessed | tf_op | source)
XLA Modules:
  0.0 44.9 jit_solution(4544178416174153866)
XLA Ops:
  0.0 0.0 copy-start.1
  0.0 0.0 copy-start.2
  0.0 0.0 copy-start.3
  0.0 0.0 copy-start.4
  0.0 1.1 %copy.9 = s32[6,16,1,1024]{3,1,2,0:T(8,128)S(1)} copy(s32[6,16,1,1024]{3,2,1,0:T(1,128)} %param.7) | data formatting | bytes 786432
  1.1 0.0 copy-done.1
  1.1 0.0 copy-done.2
  1.1 0.0 copy-done.3
  1.2 0.0 copy-done.4
  1.2 0.0 copy-start
  1.2 1.2 %copy-done = bf16[128,8,512]{2,1,0:T(8,128)(2,1)S(1)} copy-done((bf16[128,8,512]{2,1,0:T(8,128)(2,1)S(1)}, bf16[128,8,512]{2,1,0:T(8,128)(2,1)}, u32[]{:S(2)}) %copy-start) | copy-done | bytes 1048600
  2.4 41.9 %shard_map.64 = bf16[128,512]{1,0:T(8,128)(2,1)S(1)} custom-call(bf16[128,512]{1,0:T(8,128)(2,1)S(1)} %copy-done.1, s32[6,16,1024]{2,1,0:T(8,128)S(1)} %bitcast.5, s32[24,8]{1,0:T(8,128)S(1)} %bitcast.7, bf16[1024,512]{1,0:T(8,128)(2,1)S(1)} %bitcast.6, f32[6,8]{1,0:T(8,128)S(1)} %copy-done.4, bf16[128,512]{1,0:T(8,128)(2,1)S(1)} %copy-done.2), custom_call_target="tpu_custom_call" | custom-call | tf_op jit(solution)/shard_map/pallas_call | solution.py:369
  44.3 0.7 %copy.11 = bf16[128,512]{1,0:T(8,128)(2,1)} copy(bf16[128,512]{1,0:T(8,128)(2,1)S(1)} %shard_map.64) | data formatting | bytes 262144
Async XLA Ops:
  0.0 1.1 %copy-start.1 = (bf16[128,512]{1,0:T(8,128)(2,1)S(1)}, bf16[128,512]{1,0:T(8,128)(2,1)}, u32[]{:S(2)}) copy-start(bf16[128,512]{1,0:T(8,128)(2,1)} %feat.1) | copy-start | bytes 393220
  0.0 1.1 %copy-start.2 = (bf16[128,512]{1,0:T(8,128)(2,1)S(1)}, bf16[128,512]{1,0:T(8,128)(2,1)}, u32[]{:S(2)}) copy-start(bf16[128,512]{1,0:T(8,128)(2,1)} %self_hbm.1) | copy-start | bytes 393220
  0.0 1.1 %copy-start.3 = (s32[6,4,8,1]{2,3,1,0:T(1,128)S(1)}, s32[6,4,8,1]{2,3,1,0:T(1,128)}, u32[]{:S(2)}) copy-start(s32[6,4,8,1]{2,3,1,0:T(1,128)} %param.8) | copy-start | bytes 2308
  0.0 1.1 %copy-start.4 = (f32[6,8]{1,0:T(8,128)S(1)}, f32[6,8]{1,0:T(8,128)}, u32[]{:S(2)}) copy-start(f32[6,8]{1,0:T(8,128)} %coef.1) | copy-start | bytes 580
  1.2 1.2 %copy-start = (bf16[128,8,512]{2,1,0:T(8,128)(2,1)S(1)}, bf16[128,8,512]{2,1,0:T(8,128)(2,1)}, u32[]{:S(2)}) copy-start(bf16[128,8,512]{2,1,0:T(8,128)(2,1)} %param.9) | copy-start | bytes 3145732
